TPU v7x, 512 devices: a 8x2x16 block of a 8x16x16 slice. The times are simulated.
512 devices in a mesh: groups: 2 (over y), seq: 32 (over z, core), rep: 8 (over x).
Axes of the slice: x: 8, y: 2, z: 16, core: 2. Of those that a mesh axis runs over, the one named last changes fastest.
The devices are a block of a 8x16x16 slice.
Arguments:
- queries: bfloat16 [1024, 4096], P(('groups', 'seq'), 'rep'), parts along dimension 0, may hold values from -128 to 128
- keys_new: bfloat16 [1024, 1024], P(('groups', 'seq'), 'rep'), parts along dimension 0, may hold values from -4 to 4
- values_new: bfloat16 [1024, 1024], P(('groups', 'seq'), 'rep'), parts along dimension 0, may hold values from -6 to 6
- keys_past: bfloat16 [16384, 1024], P(('groups', 'seq'), 'rep'), parts along dimension 0, may hold values from -4 to 4
- values_past: bfloat16 [16384, 1024], P(('groups', 'seq'), 'rep'), parts along dimension 0, may hold values from -6 to 6
- block_order: int32 [64], P('groups'), parts along dimension 0, may hold values from 0 to 31, each once
- residual: bfloat16 [1024, 4096], P(('groups', 'seq'), 'rep'), parts along dimension 0, may hold values from -6 to 6
- out_proj: bfloat16 [4096, 4096], P('seq', 'rep'), may hold values from -0.09375 to 0.09375
- norm_gain: float32 [4096], replicated, may hold values from 0.5 to 1.5
- router: float32 [4096, 4], replicated, may hold values from -0.09375 to 0.09375
- w_gate: bfloat16 [8, 4096, 4096], P('rep', None, 'seq'), may hold values from -0.09375 to 0.09375
- w_up: bfloat16 [8, 4096, 4096], P('rep', None, 'seq'), may hold values from -0.09375 to 0.09375
- w_down: bfloat16 [8, 4096, 4096], P('rep', 'seq'), may hold values from -0.0625 to 0.0625
- expert_ids: int32 [1024, 2], P(('groups', 'seq')), parts along dimension 0, may hold values from 0 to 3, all different within a row; in each aligned block of 16 rows (0 to 15, 16 to 31, ...) at most 12 rows name the same one
Outputs:
- attended: bfloat16 [1024, 4096], P(('groups', 'seq'), 'rep'), parts along dimension 0
- layer_out: bfloat16 [1024, 4096], P(('groups', 'seq'), 'rep'), parts along dimension 0
- keys_cache: bfloat16 [1024, 1024], P(('groups', 'seq')), parts along dimension 0
- values_cache: bfloat16 [1024, 1024], P(('groups', 'seq')), parts along dimension 0
There are 2 independent parts, one for each index of `groups`. A program takes and returns all parts, laid end to end along the dimension named above; an argument that names none is the same for every part. Nothing has to cross between parts.
Inputs may be any that keep to these rules, and one draw needn't show every extreme that they name: `block_order`: each block index 0 to 32 - 1 appears once. `expert_ids`: each row names 2 different experts; in the rows of one device (aligned blocks of 16 rows) no expert is named by more than 12 rows, and in some block one expert is named by exactly 12.
All inputs are finite; a program needn't handle non-finite values.
Results may differ from a plain program's by a relative error of at most 0.011.
Values may be sent and summed in bfloat16 or wider, within the bound.
A program may use at most 64 MiB of HBM per device.

v0:
```python
import math
import jax
import jax.numpy as jnp
from jax import lax
from jax.sharding import Mesh
from jax.sharding import PartitionSpec as P

EXPERTS = 4
CAP = 12
SEQ = ("seq_0", "seq_1")
GROUPS_SEQ = ("groups", "seq_0", "seq_1")


def in_one_piece(arrays, axis, dim, along):
    both = jnp.concatenate(arrays, axis=along)
    out, at, gathered = (lax.all_gather(both, axis, axis=dim, tiled=True), 0, [])
    for a in arrays:
        gathered.append(lax.slice_in_dim(out, at, at + a.shape[along], axis=along))
        at += a.shape[along]
    return tuple(gathered)


def sent_to_all(array, axis):
    size = lax.axis_size(axis)
    return lax.all_to_all(
        jnp.broadcast_to(array[None], (size, *array.shape)), axis, 0, 0, tiled=True
    )


def laid_out(tiles, dim):
    tiles = jnp.moveaxis(tiles, 0, dim)
    shape = tiles.shape
    return tiles.reshape(*shape[:dim], shape[dim] * shape[dim + 1], *shape[dim + 2 :])


def gather_directly(array, axis, dim):
    tiles = sent_to_all(array, axis)
    return laid_out(tiles, dim)


def own_block(tiles, axes, order):
    shape = [lax.axis_size(a) for a in axes]
    tiles = tiles.reshape(*shape, *tiles.shape[1:])
    tiles = tiles.transpose(*order, *range(len(axes), tiles.ndim))
    tiles = tiles.reshape(-1, *tiles.shape[len(axes) :])
    for k in order:
        tiles = lax.psum_scatter(tiles, axes[k], scatter_dimension=0, tiled=True)
    return tiles[0]


def in_blocks(array, dim, size):
    shape = array.shape
    tiles = array.reshape(*shape[:dim], size, shape[dim] // size, *shape[dim + 1 :])
    return jnp.moveaxis(tiles, dim, 0)


def sum_by_axis(array, axes, order, dim):
    size = lax.axis_size(axes)
    return own_block(in_blocks(array, dim, size), axes, order)


def block_lookup(owners, block_order):
    width = block_order.shape[0]
    hits = owners[:, None] == jnp.arange(width, dtype=jnp.int32)[None, :]
    return jnp.sum(jnp.where(hits, block_order[None, :], 0), axis=1)


def body(
    queries,
    keys_new,
    values_new,
    keys_past,
    values_past,
    block_order,
    residual,
    out_proj,
    norm_gain,
    router,
    w_gate,
    w_up,
    w_down,
    expert_ids,
):
    seq_index = lax.axis_index(SEQ)
    rep_index = lax.axis_index("rep")
    rep_count = lax.axis_size("rep")
    tok_count = queries.shape[0]
    head_dim = keys_new.shape[1]
    q_per = queries.shape[1] // head_dim
    past_len = keys_past.shape[0]
    key_span = past_len + tok_count
    row_total = tok_count * q_per
    my_block = block_lookup(jnp.full((1,), seq_index, jnp.int32), block_order)[0]
    scaling = 1.0 / math.sqrt(head_dim)
    query_rows = queries.reshape(row_total, head_dim)
    query_pos = my_block * tok_count + jnp.arange(row_total, dtype=jnp.int32) // q_per
    keys_local = jnp.concatenate([keys_past, keys_new], axis=0)
    values_local = jnp.concatenate([values_past, values_new], axis=0)
    running = jnp.full((row_total,), -1e30, jnp.float32)
    key_piece, value_piece = in_one_piece((keys_local, values_local), SEQ, 0, 1)
    row_count = key_piece.shape[0]
    key_index = jnp.arange(row_count, dtype=jnp.int32)
    key_owner = key_index // key_span
    offset = key_index % key_span
    key_pos = block_lookup(key_owner, block_order) * tok_count + offset - past_len
    visible = (offset < past_len)[None, :] | (key_pos[None, :] <= query_pos[:, None])
    scores = jnp.dot(query_rows, key_piece.T, preferred_element_type=jnp.float32) * scaling
    highest = jnp.maximum(running, jnp.max(jnp.where(visible, scores, -1e30), axis=1))
    weights = jnp.where(visible, jnp.exp(scores - highest[:, None]), 0.0)
    totals = jnp.sum(weights, axis=1)
    numerator = jnp.dot(
        weights.astype(jnp.bfloat16), value_piece, preferred_element_type=jnp.float32
    )
    running, totals, numerator = (highest, totals, numerator)
    attn_local = (
        (numerator / totals[:, None]).reshape(tok_count, q_per * head_dim).astype(jnp.bfloat16)
    )
    attn_full, keys_cache, values_cache = (
        lax.all_gather(attn_local, "rep", axis=1, tiled=True),
        *in_one_piece((keys_new, values_new), "rep", 1, 0),
    )
    projected = jnp.dot(
        attn_full,
        lax.all_gather(out_proj, SEQ, axis=0, tiled=True),
        preferred_element_type=jnp.float32,
    )
    attended = (residual.astype(jnp.float32) + projected).astype(jnp.bfloat16)
    full_rows = gather_directly(attended, "rep", 1)
    features = full_rows.astype(jnp.float32)
    mean_square = jnp.mean(features * features, axis=1, keepdims=True)
    normed = (features * norm_gain[None, :] * lax.rsqrt(mean_square + 1e-05)).astype(jnp.bfloat16)
    logits = jnp.dot(normed.astype(jnp.float32), router, precision=lax.Precision.HIGHEST)
    expert_range = jnp.arange(EXPERTS, dtype=jnp.int32)
    first_pick = (expert_ids[:, 0:1] == expert_range[None, :]).astype(jnp.float32)
    second_pick = (expert_ids[:, 1:2] == expert_range[None, :]).astype(jnp.float32)
    share_first = jax.nn.sigmoid(
        jnp.sum(first_pick * logits, axis=1) - jnp.sum(second_pick * logits, axis=1)
    )
    token_share = share_first[:, None] * first_pick + (1.0 - share_first)[:, None] * second_pick
    member = first_pick + second_pick
    ranking = jnp.cumsum(member, axis=0) - member
    slot_range = jnp.arange(CAP, dtype=jnp.float32)
    selection = member.T[:, None, :] * (ranking.T[:, None, :] == slot_range[None, :, None]).astype(
        jnp.float32
    )
    mine_mask = (expert_range == rep_index % EXPERTS).astype(jnp.float32)
    my_selection = jnp.einsum("e,ejt->jt", mine_mask, selection)
    slot_rows = jnp.dot(
        my_selection.astype(jnp.bfloat16), normed, preferred_element_type=jnp.float32
    ).astype(jnp.bfloat16)
    gate_local = w_gate[0]
    up_local = w_up[0]
    down_local = w_down[0]
    piece = lax.all_gather(slot_rows, SEQ, axis=0, tiled=True)
    gate_part = jnp.dot(piece, gate_local, preferred_element_type=jnp.float32)
    up_part = jnp.dot(piece, up_local, preferred_element_type=jnp.float32)
    hidden_slots = (jax.nn.silu(gate_part) * up_part).astype(jnp.bfloat16)
    expert_part = sum_by_axis(
        jnp.dot(hidden_slots, down_local, preferred_element_type=jnp.float32).astype(jnp.bfloat16),
        SEQ,
        (1, 0),
        0,
    ).astype(jnp.float32)
    returned = lax.all_to_all(
        expert_part.astype(jnp.bfloat16), "rep", split_axis=1, concat_axis=0, tiled=True
    ).astype(expert_part.dtype)
    source_expert = jnp.arange(rep_count, dtype=jnp.int32) % EXPERTS
    source_pick = (source_expert[:, None] == expert_range[None, :]).astype(jnp.float32)
    combine = jnp.einsum("re,ejt,te->trj", source_pick, selection, token_share).reshape(
        tok_count, rep_count * CAP
    )
    moe_slice = jnp.dot(combine, returned, precision=lax.Precision.HIGHEST)
    layer_out = (attended.astype(jnp.float32) + moe_slice).astype(jnp.bfloat16)
    return (attended, layer_out, keys_cache, values_cache)


def solution(mesh):
    split = Mesh(
        mesh.devices.reshape(mesh.shape["groups"], 16, 2, mesh.shape["rep"]),
        ("groups", "seq_0", "seq_1", "rep"),
    )
    return jax.shard_map(
        body,
        mesh=split,
        in_specs=(
            P(GROUPS_SEQ, "rep"),
            P(GROUPS_SEQ, "rep"),
            P(GROUPS_SEQ, "rep"),
            P(GROUPS_SEQ, "rep"),
            P(GROUPS_SEQ, "rep"),
            P("groups"),
            P(GROUPS_SEQ, "rep"),
            P(SEQ, "rep"),
            P(),
            P(),
            P("rep", None, SEQ),
            P("rep", None, SEQ),
            P("rep", SEQ, None),
            P(GROUPS_SEQ, None),
        ),
        out_specs=(
            P(GROUPS_SEQ, "rep"),
            P(GROUPS_SEQ, "rep"),
            P(GROUPS_SEQ, None),
            P(GROUPS_SEQ, None),
        ),
        check_vma=False,
    )
```

profile of v0, /device:TPU:66, one launch (start us, length us, event | category | flops | bytes accessed | tf_op | source)
XLA Modules:
  0.0 435.2 jit_solution(9324647808169427397)
XLA Ops:
  7.2 0.0 copy-start
  7.2 0.1 all-gather.5.cloned.1.call-start
  7.3 1.7 maximum_maximum_fusion
  8.9 0.1 all-gather.5.cloned.1.call-update
  9.0 0.1 all-gather.7.cloned.1.call-start
  9.0 0.7 all-gather.7.cloned.1.call-update
  9.8 0.7 reshape.156
  10.5 1.3 fusion.64
  12.5 0.9 select_reduce_fusion.1
  13.5 106.4 %all-gather.5.cloned.1.call-done = bf16[8704,256]{1,0:T(8,128)(2,1)} async-done(((bf16[272,256]{1,0:T(8,128)(2,1)}), bf16[8704,256]{1,0:T(8,128)(2,1)}) %all-gather.5.cloned.1.call-update) | async-done | bytes 4456464 | tf_op jit(solution)/shard_map/all_gather | solution.py:16
  119.9 2.8 select_reduce_fusion
  122.7 0.9 fusion.5
  123.6 0.0 copy-start.6
  123.6 0.8 fusion.22
  124.5 24.7 %all_gather.16 = bf16[16,4096]{1,0:T(8,128)(2,1)S(1)} all-gather(bf16[16,512]{1,0:T(8,128)(2,1)S(1)} %convert_element_type.81), channel_id=1, replica_groups=mesh['groups'=2,'seq_0'=16,'seq_1'=2,'rep'=8] {'rep'}, dimensions={1}, use_global_device_ids=true | all-gather | bytes 147456 | tf_op jit(solution)/shard_map/all_gather | solution.py:119
  149.2 44.8 %all-gather.7.cloned.1.call-done = bf16[4096,512]{1,0:T(8,128)(2,1)} async-done(((bf16[128,512]{1,0:T(8,128)(2,1)}), bf16[4096,512]{1,0:T(8,128)(2,1)}) %all-gather.7.cloned.1.call-update) | async-done | bytes 4194320 | tf_op jit(solution)/shard_map/all_gather | solution.py:124
  194.0 2.8 fusion.16
  196.8 0.7 broadcast_in_dim.33
  197.5 7.2 %all-to-all-start = ((bf16[8,16,512]{2,1,0:T(8,128)(2,1)}), bf16[8,16,512]{2,1,0:T(8,128)(2,1)S(1)}, u32[]{:S(2)}, u32[]{:S(2)}) async-start(bf16[8,16,512]{2,1,0:T(8,128)(2,1)} %broadcast_in_dim.33), calls=%async_computation | async-start | bytes 262144 | tf_op jit(solution)/shard_map/all_to_all | solution.py:25
  204.8 8.0 %all-to-all-done = bf16[8,16,512]{2,1,0:T(8,128)(2,1)S(1)} async-done(((bf16[8,16,512]{2,1,0:T(8,128)(2,1)}), bf16[8,16,512]{2,1,0:T(8,128)(2,1)S(1)}, u32[]{:S(2)}, u32[]{:S(2)}) %all-to-all-start) | async-done | bytes 131104 | tf_op jit(solution)/shard_map/all_to_all | solution.py:25
  212.8 0.1 fusion.32
  213.0 0.3 select_reduce_fusion.2
  213.3 0.1 copy.48
  213.5 0.1 copy.49
  213.5 0.1 fusion.47
  213.7 0.9 fusion.1
  214.6 0.1 all-gather.9.cloned.1.call-update
  214.6 0.1 reduce-scatter.3.cloned.1.call-start
  214.7 68.2 %all-gather.9.cloned.1.call-done = bf16[32,12,4096]{2,1,0:T(8,128)(2,1)} async-done(((bf16[1,12,4096]{2,1,0:T(8,128)(2,1)}), bf16[32,12,4096]{2,1,0:T(8,128)(2,1)}) %all-gather.9.cloned.1.call-update) | async-done | bytes 3145744 | tf_op jit(solution)/shard_map/all_gather | solution.py:154
  282.9 5.6 %reshape.160 = bf16[384,4096]{1,0:T(8,128)(2,1)} reshape(bf16[32,12,4096]{2,1,0:T(8,128)(2,1)} %all-gather.9.cloned.1.call-done) | data formatting | bytes 6291456
  288.5 2.9 fusion.30
  291.5 7.0 %convolution_convert_fusion = bf16[384,4096]{1,0:T(8,128)(2,1)} fusion(bf16[384,4096]{1,0:T(8,128)(2,1)} %reshape.160, bf16[1,128,4096]{2,1,0:T(8,128)(2,1)S(1)} %copy-done, bf16[1,4096,128]{2,1,0:T(8,128)(2,1)S(1)} %copy-done.2, f32[384,128]{1,0:T(8,128)S(1)} %fusion.30), kind=kOutput, calls=%fused_computation.2 | convolution fusion | flops 807174144 | bytes 8585216 | tf_op jit(solution)/shard_map/dot_general | solution.py:159
  298.5 5.5 %reshape_reshape.3 = bf16[16,2,12,4096]{3,2,1,0:T(8,128)(2,1)} reshape(bf16[384,4096]{1,0:T(8,128)(2,1)} %convolution_convert_fusion) | data formatting | bytes 6291456 | tf_op jit(solution)/shard_map/reshape;reshape | solution.py:43
  304.0 5.6 %copy.51 = bf16[2,16,12,4096]{3,1,0,2:T(8,128)(2,1)} copy(bf16[2,16,12,4096]{3,2,0,1:T(8,128)(2,1)} %bitcast.62) | data formatting | bytes 6291456 | tf_op jit(solution)/shard_map/transpose | solution.py:44
  309.6 0.1 reduce-scatter.3.cloned.1.call-update
  309.7 0.2 reduce-scatter.5.cloned.1.call-start
  309.9 19.5 %reduce-scatter.3.cloned.1.call-done = bf16[16,12,4096]{2,0,1:T(8,128)(2,1)} async-done(((bf16[32,12,4096]{2,0,1:T(8,128)(2,1)}), bf16[16,12,4096]{2,0,1:T(8,128)(2,1)}) %reduce-scatter.3.cloned.1.call-update) | async-done | bytes 1572880 | tf_op jit(solution)/shard_map/reduce_scatter | solution.py:47
  329.5 3.7 copy.52
  333.1 0.1 reduce-scatter.5.cloned.1.call-update
  333.2 22.3 %all_gather.19 = bf16[32,1024]{1,0:T(8,128)(2,1)S(1)} all-gather(bf16[32,128]{1,0:T(8,128)(2,1)S(1)} %pad_maximum_fusion), channel_id=1, replica_groups=mesh['groups'=2,'seq_0'=16,'seq_1'=2,'rep'=8] {'rep'}, dimensions={1}, use_global_device_ids=true | all-gather | bytes 73728 | tf_op jit(solution)/shard_map/all_gather | solution.py:16
  355.6 0.6 fusion.72
  356.2 54.9 %reduce-scatter.5.cloned.1.call-done = bf16[1,12,4096]{2,1,0:T(8,128)(2,1)} async-done(((bf16[16,12,4096]{2,1,0:T(8,128)(2,1)}), bf16[1,12,4096]{2,1,0:T(8,128)(2,1)}) %reduce-scatter.5.cloned.1.call-update) | async-done | bytes 98320 | tf_op jit(solution)/shard_map/reduce_scatter | solution.py:47
  411.1 0.9 copy.57
  412.0 0.7 copy.53
  412.7 7.4 %all-to-all-start.1 = ((bf16[12,8,512]{2,0,1:T(8,128)(2,1)}), bf16[12,8,512]{2,0,1:T(8,128)(2,1)S(1)}, u32[]{:S(2)}, u32[]{:S(2)}) async-start(bf16[12,8,512]{2,0,1:T(8,128)(2,1)} %copy.53), calls=%async_computation.3 | async-start | bytes 262144 | tf_op jit(solution)/shard_map/all_to_all | solution.py:164
  420.2 0.2 convolution_bitcast_fusion
  420.4 7.4 %all-to-all-done.1 = bf16[12,8,512]{2,0,1:T(8,128)(2,1)S(1)} async-done(((bf16[12,8,512]{2,0,1:T(8,128)(2,1)}), bf16[12,8,512]{2,0,1:T(8,128)(2,1)S(1)}, u32[]{:S(2)}, u32[]{:S(2)}) %all-to-all-start.1) | async-done | bytes 98336 | tf_op jit(solution)/shard_map/all_to_all | solution.py:164
  427.8 0.8 fusion.15
  (38 shorter events, 0.3 us)
Async XLA Ops:
  7.2 284.3 %copy-start = (bf16[1,128,4096]{2,1,0:T(8,128)(2,1)S(1)}, bf16[1,128,4096]{2,1,0:T(8,128)(2,1)}, u32[]{:S(2)}) copy-start(bf16[1,128,4096]{2,1,0:T(8,128)(2,1)} %param.26) | copy-start | bytes 3145732
  7.2 112.7 %all-gather.5.cloned.1.call-start = ((), (), s32[]{:S(2)}) async-start(), calls=%async_computation.4 | async-start | bytes 4595712 | tf_op jit(solution)/shard_map/all_gather | solution.py:16
  9.0 185.0 %all-gather.7.cloned.1.call-start = ((), (), s32[]{:S(2)}) async-start(), calls=%async_computation.5 | async-start | bytes 4325376 | tf_op jit(solution)/shard_map/all_gather | solution.py:124
  119.9 3.7 copy-start.10
  123.6 70.4 %copy-start.6 = (bf16[16,512]{1,0:T(8,128)(2,1)S(1)}, bf16[16,512]{1,0:T(8,128)(2,1)}, u32[]{:S(2)}) copy-start(bf16[16,512]{1,0:T(8,128)(2,1)} %param.20) | copy-start | bytes 49156
  149.2 55.5 %copy-start.9 = (s32[16,2]{0,1:T(2,128)S(1)}, s32[16,2]{0,1:T(2,128)}, u32[]{:S(2)}) copy-start(s32[16,2]{0,1:T(2,128)} %param.27) | copy-start | bytes 388
  149.2 63.7 %copy-start.4 = (f32[4096,4]{0,1:T(4,128)S(1)}, f32[4096,4]{0,1:T(4,128)}, u32[]{:S(2)}) copy-start(f32[4096,4]{0,1:T(4,128)} %param.23) | copy-start | bytes 196612
  149.2 63.8 %copy-start.5 = (f32[4096]{0:T(1024)S(1)}, f32[4096]{0:T(1024)}, u32[]{:S(2)}) copy-start(f32[4096]{0:T(1024)} %param.22) | copy-start | bytes 49156
  196.8 231.0 %copy-start.3 = (bf16[16,512]{1,0:T(8,128)(2,1)}, bf16[16,512]{1,0:T(8,128)(2,1)S(1)}, u32[]{:S(2)}) copy-start(bf16[16,512]{1,0:T(8,128)(2,1)S(1)} %fusion.16) | copy-start | bytes 49156
  197.5 15.2 %all-to-all-start = ((bf16[8,16,512]{2,1,0:T(8,128)(2,1)}), bf16[8,16,512]{2,1,0:T(8,128)(2,1)S(1)}, u32[]{:S(2)}, u32[]{:S(2)}) async-start(bf16[8,16,512]{2,1,0:T(8,128)(2,1)} %broadcast_in_dim.33), calls=%async_computation | async-start | bytes 262144 | tf_op jit(solution)/shard_map/all_to_all | solution.py:25
  204.7 78.2 %all-gather.9.cloned.1.call-start = ((), (), s32[]{:S(2)}) async-start(), calls=%async_computation.8 | async-start | bytes 4325376 | tf_op jit(solution)/shard_map/all_gather | solution.py:154
  214.6 73.9 %copy-start.1 = (bf16[1,4096,128]{2,1,0:T(8,128)(2,1)S(1)}, bf16[1,4096,128]{2,1,0:T(8,128)(2,1)}, u32[]{:S(2)}) copy-start(bf16[1,4096,128]{2,1,0:T(8,128)(2,1)} %param.24) | copy-start | bytes 3145732
  214.6 114.8 %reduce-scatter.3.cloned.1.call-start = ((), (), s32[]{:S(2)}) async-start(), calls=%async_computation.6 | async-start | bytes 4718592 | tf_op jit(solution)/shard_map/reduce_scatter | solution.py:47
  288.5 3.0 copy-start.2
  309.7 23.5 %copy-start.7 = (bf16[16,128]{1,0:T(8,128)(2,1)S(1)}, bf16[16,128]{1,0:T(8,128)(2,1)}, u32[]{:S(2)}) copy-start(bf16[16,128]{1,0:T(8,128)(2,1)} %param.16) | copy-start | bytes 12292
  309.7 23.5 %copy-start.8 = (bf16[16,128]{1,0:T(8,128)(2,1)S(1)}, bf16[16,128]{1,0:T(8,128)(2,1)}, u32[]{:S(2)}) copy-start(bf16[16,128]{1,0:T(8,128)(2,1)} %param.15) | copy-start | bytes 12292
  309.7 101.4 %reduce-scatter.5.cloned.1.call-start = ((), (), s32[]{:S(2)}) async-start(), calls=%async_computation.7 | async-start | bytes 2228224 | tf_op jit(solution)/shard_map/reduce_scatter | solution.py:47
  412.7 15.1 %all-to-all-start.1 = ((bf16[12,8,512]{2,0,1:T(8,128)(2,1)}), bf16[12,8,512]{2,0,1:T(8,128)(2,1)S(1)}, u32[]{:S(2)}, u32[]{:S(2)}) async-start(bf16[12,8,512]{2,0,1:T(8,128)(2,1)} %copy.53), calls=%async_computation.3 | async-start | bytes 262144 | tf_op jit(solution)/shard_map/all_to_all | solution.py:164
Sparse Core Ops, SparseCore 0:
  10.2 109.7 all-gather.4
  122.1 71.8 all-gather.6
  214.7 68.1 all-gather.8
  309.8 19.6 reduce-scatter.2
  333.3 77.7 reduce-scatter.4
where the time goes:
time: 436 us; the launch traced here: 435 us
  waiting for transfers between devices  310 us (71%)
  blocking collectives  47 us (11%)
  local copies, waits for them, and re-layouts  24.3 us (6%)
  matrix products  18.8 us (4%)
  starting transfers between devices  15.1 us (3%)
  between operations  14.7 us (3%)
  other arithmetic  5.04 us (1%)
    all_gather x1, waiting for transfers between devices, in_one_piece(): lax.all_gather(both, axis, axis=dim, tiled=True)  106 us
    reduce_scatter x2, waiting for transfers between devices, own_block(): tiles = lax.psum_scatter(tiles, axes[k], scatter_dimension=0, tiled=True)  74.4 us
    all_gather x1, waiting for transfers between devices, body(): piece = lax.all_gather(slot_rows, SEQ, axis=0, tiled=True)  68.2 us
    all_gather x1, waiting for transfers between devices, body(): lax.all_gather(out_proj, SEQ, axis=0, tiled=True)  44.8 us
    all_gather x1, blocking collectives, body(): lax.all_gather(attn_local, 'rep', axis=1, tiled=True)  24.7 us
    all_gather x1, blocking collectives, in_one_piece(): lax.all_gather(both, axis, axis=dim, tiled=True)  22.3 us
  transfers between devices with their start and end apart: 7, of which 7 were waited for; matrix products, arithmetic and copies ran while one was open for 2% of the time, Pallas kernels for 0%

commit v1 on v0

--- a/solution.py
+++ b/solution.py
@@ -121,7 +121,9 @@
     )
     projected = jnp.dot(
         attn_full,
-        lax.all_gather(out_proj, SEQ, axis=0, tiled=True),
+        jnp.concatenate(
+            lax.all_to_all(jnp.stack([out_proj] * lax.axis_size(SEQ)), SEQ, 0, 0), axis=0
+        ),
         preferred_element_type=jnp.float32,
     )
     attended = (residual.astype(jnp.float32) + projected).astype(jnp.bfloat16)

time: 436 us -> 506 us (1.16)
  starting transfers between devices: 15.1 us -> 64.5 us
  waiting for transfers between devices: 310 us -> 331 us
    all_gather x1, waiting for transfers between devices: 106 us -> 158 us  [in_one_piece(): lax.all_gather(both, axis, axis=dim, tiled=True)]
    all_gather x1 -> x0, waiting for transfers between devices: 44.8 us -> none  [body(): lax.all_gather(out_proj, SEQ, axis=0, tiled=True)]
    all_to_all x0 -> x1, starting transfers between devices: none -> 44.6 us  [body(): lax.all_to_all(jnp.stack([out_proj] * lax.axis_size(SEQ)), SEQ, 0, 0)]
    all_to_all x0 -> x1, waiting for transfers between devices: none -> 16.6 us  [body(): lax.all_to_all(jnp.stack([out_proj] * lax.axis_size(SEQ)), SEQ, 0, 0)]
  transfers between devices with their start and end apart: 7 -> 7, of which waited for: 7 -> 7; matrix products, arithmetic and copies ran while one was open for 2% -> 1% of each run, Pallas kernels for 0% -> 0%
where the time goes in v1:
time: 506 us; the launch traced here: 505 us
  waiting for transfers between devices  331 us (65%)
  starting transfers between devices  64.5 us (13%)
  blocking collectives  46.3 us (9%)
  local copies, waits for them, and re-layouts  27 us (5%)
  matrix products  18.8 us (4%)
  between operations  14.7 us (3%)
    all_gather x1, waiting for transfers between devices, in_one_piece(): lax.all_gather(both, axis, axis=dim, tiled=True)  158 us
    reduce_scatter x2, waiting for transfers between devices, own_block(): tiles = lax.psum_scatter(tiles, axes[k], scatter_dimension=0, tiled=True)  74.6 us
    all_gather x1, waiting for transfers between devices, body(): piece = lax.all_gather(slot_rows, SEQ, axis=0, tiled=True)  66.1 us
    all_to_all x1, starting transfers between devices, body(): lax.all_to_all(jnp.stack([out_proj] * lax.axis_size(SEQ)), SEQ, 0, 0)  44.6 us
    all_gather x1, blocking collectives, body(): lax.all_gather(attn_local, 'rep', axis=1, tiled=True)  24 us
    all_gather x1, blocking collectives, in_one_piece(): lax.all_gather(both, axis, axis=dim, tiled=True)  22.3 us
    all_to_all x1, waiting for transfers between devices, body(): lax.all_to_all(jnp.stack([out_proj] * lax.axis_size(SEQ)), SEQ, 0, 0)  16.6 us
    all_to_all x1, starting transfers between devices, sent_to_all(): lax.all_to_all(jnp.broadcast_to(array[None], (size, *array.shape)), axis,...  12.1 us
  transfers between devices with their start and end apart: 7, of which 7 were waited for; matrix products, arithmetic and copies ran while one was open for 1% of the time, Pallas kernels for 0%

profile of v1, /device:TPU:66, one launch (start us, length us, event | category | flops | bytes accessed | tf_op | source)
XLA Modules:
  0.0 504.9 jit_solution(5374908904002814061)
XLA Ops:
  7.2 0.0 copy-start
  7.2 3.4 stack.2
  10.6 0.0 copy-start.11
  10.7 0.0 copy-start.13
  10.7 44.6 %all-to-all-start = ((bf16[32,128,512]{2,1,0:T(8,128)(2,1)}), bf16[32,128,512]{2,1,0:T(8,128)(2,1)}, u32[]{:S(2)}, u32[]{:S(2)}) async-start(bf16[32,128,512]{2,1,0:T(8,128)(2,1)} %stack.2), calls=%async_computation | async-start | bytes 8388608 | tf_op jit(solution)/shard_map/all_to_all | solution.py:125
  55.3 0.1 all-gather.4.cloned.1.call-start
  55.4 0.7 maximum_maximum_fusion
  56.1 0.1 all-gather.4.cloned.1.call-update
  56.2 0.6 fusion.64
  57.5 0.3 select_reduce_fusion.1
  57.8 158.2 %all-gather.4.cloned.1.call-done = bf16[8704,256]{1,0:T(8,128)(2,1)} async-done(((bf16[272,256]{1,0:T(8,128)(2,1)}), bf16[8704,256]{1,0:T(8,128)(2,1)}) %all-gather.4.cloned.1.call-update) | async-done | bytes 4456464 | tf_op jit(solution)/shard_map/all_gather | solution.py:16
  216.0 2.8 select_reduce_fusion
  218.8 0.9 fusion.5
  219.7 0.8 fusion.22
  220.6 24.0 %all_gather.13 = bf16[16,4096]{1,0:T(8,128)(2,1)S(1)} all-gather(bf16[16,512]{1,0:T(8,128)(2,1)S(1)} %convert_element_type.81), channel_id=1, replica_groups=mesh['groups'=2,'seq_0'=16,'seq_1'=2,'rep'=8] {'rep'}, dimensions={1}, use_global_device_ids=true | all-gather | bytes 147456 | tf_op jit(solution)/shard_map/all_gather | solution.py:119
  244.6 16.6 %all-to-all-done = bf16[32,128,512]{2,1,0:T(8,128)(2,1)} async-done(((bf16[32,128,512]{2,1,0:T(8,128)(2,1)}), bf16[32,128,512]{2,1,0:T(8,128)(2,1)}, u32[]{:S(2)}, u32[]{:S(2)}) %all-to-all-start) | async-done | bytes 4194336 | tf_op jit(solution)/shard_map/all_to_all | solution.py:125
  261.2 2.9 fusion.16
  264.0 0.7 broadcast_in_dim.33
  264.7 12.1 %all-to-all-start.1 = ((bf16[8,16,512]{2,1,0:T(8,128)(2,1)}), bf16[8,16,512]{2,1,0:T(8,128)(2,1)S(1)}, u32[]{:S(2)}, u32[]{:S(2)}) async-start(bf16[8,16,512]{2,1,0:T(8,128)(2,1)} %broadcast_in_dim.33), calls=%async_computation.1 | async-start | bytes 262144 | tf_op jit(solution)/shard_map/all_to_all | solution.py:25
  276.8 7.7 %all-to-all-done.1 = bf16[8,16,512]{2,1,0:T(8,128)(2,1)S(1)} async-done(((bf16[8,16,512]{2,1,0:T(8,128)(2,1)}), bf16[8,16,512]{2,1,0:T(8,128)(2,1)S(1)}, u32[]{:S(2)}, u32[]{:S(2)}) %all-to-all-start.1) | async-done | bytes 131104 | tf_op jit(solution)/shard_map/all_to_all | solution.py:25
  284.5 0.1 fusion.32
  284.7 0.3 select_reduce_fusion.2
  285.0 0.1 copy.48
  285.2 0.1 copy.49
  285.3 0.1 fusion.47
  285.4 0.9 fusion.1
  286.3 0.1 all-gather.6.cloned.1.call-update
  286.3 0.2 reduce-scatter.3.cloned.1.call-start
  286.6 66.1 %all-gather.6.cloned.1.call-done = bf16[32,12,4096]{2,1,0:T(8,128)(2,1)} async-done(((bf16[1,12,4096]{2,1,0:T(8,128)(2,1)}), bf16[32,12,4096]{2,1,0:T(8,128)(2,1)}) %all-gather.6.cloned.1.call-update) | async-done | bytes 3145744 | tf_op jit(solution)/shard_map/all_gather | solution.py:156
  352.7 5.6 %reshape.166 = bf16[384,4096]{1,0:T(8,128)(2,1)} reshape(bf16[32,12,4096]{2,1,0:T(8,128)(2,1)} %all-gather.6.cloned.1.call-done) | data formatting | bytes 6291456
  358.3 3.0 fusion.30
  361.3 7.0 %convolution_convert_fusion = bf16[384,4096]{1,0:T(8,128)(2,1)} fusion(bf16[384,4096]{1,0:T(8,128)(2,1)} %reshape.166, bf16[1,128,4096]{2,1,0:T(8,128)(2,1)S(1)} %copy-done, bf16[1,4096,128]{2,1,0:T(8,128)(2,1)S(1)} %copy-done.2, f32[384,128]{1,0:T(8,128)S(1)} %fusion.30), kind=kOutput, calls=%fused_computation.2 | convolution fusion | flops 807174144 | bytes 8585216 | tf_op jit(solution)/shard_map/dot_general | solution.py:161
  368.3 5.5 %reshape_reshape.3 = bf16[16,2,12,4096]{3,2,1,0:T(8,128)(2,1)} reshape(bf16[384,4096]{1,0:T(8,128)(2,1)} %convolution_convert_fusion) | data formatting | bytes 6291456 | tf_op jit(solution)/shard_map/reshape;reshape | solution.py:43
  373.8 5.6 %copy.51 = bf16[2,16,12,4096]{3,1,0,2:T(8,128)(2,1)} copy(bf16[2,16,12,4096]{3,2,0,1:T(8,128)(2,1)} %bitcast.63) | data formatting | bytes 6291456 | tf_op jit(solution)/shard_map/transpose | solution.py:44
  379.4 0.1 reduce-scatter.3.cloned.1.call-update
  379.4 0.1 reduce-scatter.5.cloned.1.call-start
  379.5 19.7 %reduce-scatter.3.cloned.1.call-done = bf16[16,12,4096]{2,0,1:T(8,128)(2,1)} async-done(((bf16[32,12,4096]{2,0,1:T(8,128)(2,1)}), bf16[16,12,4096]{2,0,1:T(8,128)(2,1)}) %reduce-scatter.3.cloned.1.call-update) | async-done | bytes 1572880 | tf_op jit(solution)/shard_map/reduce_scatter | solution.py:47
  399.3 3.6 copy.52
  402.9 0.1 reduce-scatter.5.cloned.1.call-update
  403.0 22.3 %all_gather.15 = bf16[32,1024]{1,0:T(8,128)(2,1)S(1)} all-gather(bf16[32,128]{1,0:T(8,128)(2,1)S(1)} %pad_maximum_fusion), channel_id=1, replica_groups=mesh['groups'=2,'seq_0'=16,'seq_1'=2,'rep'=8] {'rep'}, dimensions={1}, use_global_device_ids=true | all-gather | bytes 73728 | tf_op jit(solution)/shard_map/all_gather | solution.py:16
  425.3 0.6 fusion.72
  426.0 54.8 %reduce-scatter.5.cloned.1.call-done = bf16[1,12,4096]{2,1,0:T(8,128)(2,1)} async-done(((bf16[16,12,4096]{2,1,0:T(8,128)(2,1)}), bf16[1,12,4096]{2,1,0:T(8,128)(2,1)}) %reduce-scatter.5.cloned.1.call-update) | async-done | bytes 98320 | tf_op jit(solution)/shard_map/reduce_scatter | solution.py:47
  480.8 0.9 copy.57
  481.8 0.7 copy.53
  482.4 7.5 %all-to-all-start.2 = ((bf16[12,8,512]{2,0,1:T(8,128)(2,1)}), bf16[12,8,512]{2,0,1:T(8,128)(2,1)S(1)}, u32[]{:S(2)}, u32[]{:S(2)}) async-start(bf16[12,8,512]{2,0,1:T(8,128)(2,1)} %copy.53), calls=%async_computation.4 | async-start | bytes 262144 | tf_op jit(solution)/shard_map/all_to_all | solution.py:166
  489.9 0.2 convolution_bitcast_fusion
  490.1 7.4 %all-to-all-done.2 = bf16[12,8,512]{2,0,1:T(8,128)(2,1)S(1)} async-done(((bf16[12,8,512]{2,0,1:T(8,128)(2,1)}), bf16[12,8,512]{2,0,1:T(8,128)(2,1)S(1)}, u32[]{:S(2)}, u32[]{:S(2)}) %all-to-all-start.2) | async-done | bytes 98336 | tf_op jit(solution)/shard_map/all_to_all | solution.py:166
  497.6 0.8 fusion.15
  (46 shorter events, 0.3 us)
Async XLA Ops:
  7.2 354.1 %copy-start = (bf16[1,128,4096]{2,1,0:T(8,128)(2,1)S(1)}, bf16[1,128,4096]{2,1,0:T(8,128)(2,1)}, u32[]{:S(2)}) copy-start(bf16[1,128,4096]{2,1,0:T(8,128)(2,1)} %param.26) | copy-start | bytes 3145732
  10.6 44.7 %copy-start.4 = (bf16[256,128]{1,0:T(8,128)(2,1)S(1)}, bf16[256,128]{1,0:T(8,128)(2,1)}, u32[]{:S(2)}) copy-start(bf16[256,128]{1,0:T(8,128)(2,1)} %param.18) | copy-start | bytes 196612
  10.6 44.7 %copy-start.5 = (bf16[256,128]{1,0:T(8,128)(2,1)S(1)}, bf16[256,128]{1,0:T(8,128)(2,1)}, u32[]{:S(2)}) copy-start(bf16[256,128]{1,0:T(8,128)(2,1)} %param.17) | copy-start | bytes 196612
  10.6 44.7 %copy-start.9 = (bf16[16,128]{1,0:T(8,128)(2,1)S(1)}, bf16[16,128]{1,0:T(8,128)(2,1)}, u32[]{:S(2)}) copy-start(bf16[16,128]{1,0:T(8,128)(2,1)} %param.16) | copy-start | bytes 12292
  10.6 44.7 %copy-start.10 = (bf16[16,128]{1,0:T(8,128)(2,1)S(1)}, bf16[16,128]{1,0:T(8,128)(2,1)}, u32[]{:S(2)}) copy-start(bf16[16,128]{1,0:T(8,128)(2,1)} %param.15) | copy-start | bytes 12292
  10.6 45.5 %copy-start.11 = (bf16[16,512]{1,0:T(8,128)(2,1)S(1)}, bf16[16,512]{1,0:T(8,128)(2,1)}, u32[]{:S(2)}) copy-start(bf16[16,512]{1,0:T(8,128)(2,1)} %param.14) | copy-start | bytes 49156
  10.7 45.5 %copy-start.13 = (s32[32]{0:T(128)S(1)}, s32[32]{0:T(128)}, u32[]{:S(2)}) copy-start(s32[32]{0:T(128)} %param.19) | copy-start | bytes 388
  10.7 250.5 %all-to-all-start = ((bf16[32,128,512]{2,1,0:T(8,128)(2,1)}), bf16[32,128,512]{2,1,0:T(8,128)(2,1)}, u32[]{:S(2)}, u32[]{:S(2)}) async-start(bf16[32,128,512]{2,1,0:T(8,128)(2,1)} %stack.2), calls=%async_computation | async-start | bytes 8388608 | tf_op jit(solution)/shard_map/all_to_all | solution.py:125
  55.3 160.7 %all-gather.4.cloned.1.call-start = ((), (), s32[]{:S(2)}) async-start(), calls=%async_computation.5 | async-start | bytes 4595712 | tf_op jit(solution)/shard_map/all_gather | solution.py:16
  216.0 3.7 copy-start.14
  219.7 41.4 %copy-start.8 = (bf16[16,512]{1,0:T(8,128)(2,1)S(1)}, bf16[16,512]{1,0:T(8,128)(2,1)}, u32[]{:S(2)}) copy-start(bf16[16,512]{1,0:T(8,128)(2,1)} %param.20) | copy-start | bytes 49156
  261.1 15.6 %copy-start.12 = (s32[16,2]{0,1:T(2,128)S(1)}, s32[16,2]{0,1:T(2,128)}, u32[]{:S(2)}) copy-start(s32[16,2]{0,1:T(2,128)} %param.27) | copy-start | bytes 388
  261.2 23.5 %copy-start.6 = (f32[4096,4]{0,1:T(4,128)S(1)}, f32[4096,4]{0,1:T(4,128)}, u32[]{:S(2)}) copy-start(f32[4096,4]{0,1:T(4,128)} %param.23) | copy-start | bytes 196612
  261.2 23.5 %copy-start.7 = (f32[4096]{0:T(1024)S(1)}, f32[4096]{0:T(1024)}, u32[]{:S(2)}) copy-start(f32[4096]{0:T(1024)} %param.22) | copy-start | bytes 49156
  264.0 233.5 %copy-start.3 = (bf16[16,512]{1,0:T(8,128)(2,1)}, bf16[16,512]{1,0:T(8,128)(2,1)S(1)}, u32[]{:S(2)}) copy-start(bf16[16,512]{1,0:T(8,128)(2,1)S(1)} %fusion.16) | copy-start | bytes 49156
  264.7 19.8 %all-to-all-start.1 = ((bf16[8,16,512]{2,1,0:T(8,128)(2,1)}), bf16[8,16,512]{2,1,0:T(8,128)(2,1)S(1)}, u32[]{:S(2)}, u32[]{:S(2)}) async-start(bf16[8,16,512]{2,1,0:T(8,128)(2,1)} %broadcast_in_dim.33), calls=%async_computation.1 | async-start | bytes 262144 | tf_op jit(solution)/shard_map/all_to_all | solution.py:25
  276.8 76.0 %all-gather.6.cloned.1.call-start = ((), (), s32[]{:S(2)}) async-start(), calls=%async_computation.8 | async-start | bytes 4325376 | tf_op jit(solution)/shard_map/all_gather | solution.py:156
  286.3 72.0 %copy-start.1 = (bf16[1,4096,128]{2,1,0:T(8,128)(2,1)S(1)}, bf16[1,4096,128]{2,1,0:T(8,128)(2,1)}, u32[]{:S(2)}) copy-start(bf16[1,4096,128]{2,1,0:T(8,128)(2,1)} %param.24) | copy-start | bytes 3145732
  286.3 112.9 %reduce-scatter.3.cloned.1.call-start = ((), (), s32[]{:S(2)}) async-start(), calls=%async_computation.6 | async-start | bytes 4718592 | tf_op jit(solution)/shard_map/reduce_scatter | solution.py:47
  358.3 3.0 copy-start.2
  379.4 101.4 %reduce-scatter.5.cloned.1.call-start = ((), (), s32[]{:S(2)}) async-start(), calls=%async_computation.7 | async-start | bytes 2228224 | tf_op jit(solution)/shard_map/reduce_scatter | solution.py:47
  482.4 15.1 %all-to-all-start.2 = ((bf16[12,8,512]{2,0,1:T(8,128)(2,1)}), bf16[12,8,512]{2,0,1:T(8,128)(2,1)S(1)}, u32[]{:S(2)}, u32[]{:S(2)}) async-start(bf16[12,8,512]{2,0,1:T(8,128)(2,1)} %copy.53), calls=%async_computation.4 | async-start | bytes 262144 | tf_op jit(solution)/shard_map/all_to_all | solution.py:166
Sparse Core Ops, SparseCore 0:
  58.3 157.7 all-gather.3
  286.5 66.2 all-gather.5
  379.6 19.6 reduce-scatter.2
  403.1 77.6 reduce-scatter.4
